TPU v7x, 32 devices: a whole 2x2x4 slice. The times are simulated.
32 devices in a mesh: patch: 8 (over y, x, core), rhs: 4 (over z).
Axes of the slice: x: 2, y: 2, z: 4, core: 2. Of those that a mesh axis runs over, the one named last changes fastest.
Arguments:
- rhs_vectors: float32 [64, 16, 384], P('patch', 'rhs'), may hold values from -8 to 8
- near_blocks: bfloat16 [64, 4, 384, 384], P('patch'), may hold values from -1 to 5, as said below
- neighbours: int32 [64, 4], P('patch'), may hold values from 0 to 63, as said below
- up_maps: float32 [64, 64, 384], P('patch'), may hold values from -0.3125 to 0.3125
- shift_up: float32 [64, 64, 64], P('patch'), may hold values from -0.25 to 0.25
- far_lists: int32 [8, 4], P('patch'), may hold values from 0 to 7, as said below
- translations: float32 [8, 4, 64, 64], P('patch'), may hold values from -0.375 to 0.375
- shift_down: float32 [64, 64, 64], P('patch'), may hold values from -0.75 to 0.75
- down_maps: float32 [64, 384, 64], P('patch'), may hold values from -0.375 to 0.375
Outputs:
- solution: float32 [64, 16, 384], P('patch', 'rhs')
- residual: float32 [64, 16, 384], P('patch', 'rhs')
Inputs may be any that keep to these rules, and one draw needn't show every extreme that they name: `neighbours`: entry 0 of each row is the patch itself; every other entry names a patch of the same cell or of the cell just before or just after it, cyclically. `far_lists`: entry 0 of each row names the cell just before or just after the row's own cell, cyclically, and for cell 0 the cell just before it; every other entry names a cell other than the row's own. `near_blocks`: the blocks keep the operator's symmetric part positive definite.
All inputs are finite; a program needn't handle non-finite values.
Results may differ from a plain program's by a relative error of at most 0.008.
The roundings to bfloat16 on the way count: a program that leaves them out, or rounds other values in their place, can miss the bound.
Values may be sent and summed in bfloat16 or wider, within the bound.
A program may use at most 64 MiB of HBM per device.

v0:
```python
import functools

import jax
import jax.numpy as jnp
from jax import lax
from jax.experimental import pallas as pl
from jax.experimental.pallas import tpu as pltpu
from jax.sharding import PartitionSpec as P

ITERS = 2
HIGH = lax.Precision.HIGHEST
MESH = pl.DeviceIdType.MESH


def nt(a, b, precision=HIGH):
    return lax.dot_general(
        a, b, (((1,), (1,)), ((), ())), precision=precision, preferred_element_type=jnp.float32
    )


def wrap(i, n):
    return jnp.where(i >= n, i - n, i)


def nn(a, b):
    return lax.dot_general(
        a, b, (((1,), (0,)), ((), ())), precision=HIGH, preferred_element_type=jnp.float32
    )


def split(x):
    high = x.astype(jnp.bfloat16)
    return high, (x - high.astype(jnp.float32)).astype(jnp.bfloat16)


def eliminate(systems):
    n = systems[0].shape[0]
    for k in range(n):
        done = []
        for a in systems:
            rows = lax.broadcasted_iota(jnp.int32, a.shape, 0)
            row = a[k : k + 1, :] / a[k : k + 1, k : k + 1]
            done.append(jnp.where(rows == k, row, a - a[:, k : k + 1] * row))
        systems = done
    return systems


def kernel(
    cells,
    zs,
    rhs_hbm,
    near_hbm,
    neigh,
    up_hbm,
    su_hbm,
    far,
    tr_hbm,
    sd_hbm,
    dn_hbm,
    sol_out,
    res_out,
    rhs,
    blocks,
    up,
    su,
    tr,
    sd,
    dn,
    gcat,
    ucat,
    halo,
    moment,
    mom_out,
    own_dir,
    own_img,
    own_res,
    gathered,
    images,
    full_r,
    full_i,
    full_d,
    strip_out,
    strips,
    new_out,
    news,
    near_sem,
    map_sem,
    halo_s,
    halo_r,
    mom_s,
    mom_r,
    gat_s,
    gat_r,
    img_s,
    img_r,
    strip_s,
    strip_r,
    new_s,
    new_r,
):
    c = lax.axis_index("patch")
    z = lax.axis_index("rhs")
    patches, cols, width = rhs.shape
    terms = su.shape[1]
    total_cols = cols * zs
    total = patches * cells
    devices = cells * zs
    me = c * zs + z

    maps = [(up_hbm, up), (su_hbm, su), (sd_hbm, sd), (dn_hbm, dn), (tr_hbm, tr), (rhs_hbm, rhs)]
    map_copies = [
        pltpu.make_async_copy(src, dst, map_sem.at[i]) for i, (src, dst) in enumerate(maps)
    ]
    map_copies[5].start()
    for copy in map_copies[:2]:
        copy.start()

    barrier = pltpu.get_barrier_semaphore()

    def everyone(body):
        for dz in range(zs):
            tz = wrap(z + dz, zs)
            for dc in range(0 if dz else 1, cells):
                body(wrap(c + dc, cells), tz)

    everyone(
        lambda tc, tz: pl.semaphore_signal(
            barrier, inc=1, device_id=(tc, tz), device_id_type=MESH
        )
    )

    def near_copy(p):
        return pltpu.make_async_copy(near_hbm.at[p], blocks.at[p], near_sem.at[p])

    def start_near(p, carry):
        near_copy(p).start()
        return carry

    lax.fori_loop(0, patches, start_near, 0)
    for copy in map_copies[2:5]:
        copy.start()

    def cell_of(i):
        return wrap(c + i, cells)

    def halo_copy(it, src, side):
        target = cell_of(1 if side == 0 else cells - 1)
        dst = halo.at[it, pl.ds(0 if side == 0 else 2 * patches, patches)]
        return pltpu.make_async_remote_copy(
            src_ref=src,
            dst_ref=dst,
            send_sem=halo_s.at[it, side],
            recv_sem=halo_r.at[it, side],
            device_id=(target, z),
            device_id_type=MESH,
        )

    def moment_copy(it, target, slot):
        return pltpu.make_async_remote_copy(
            src_ref=mom_out.at[it],
            dst_ref=moment.at[it, slot],
            send_sem=mom_s.at[it, target],
            recv_sem=mom_r.at[it, slot],
            device_id=(target, z),
            device_id_type=MESH,
        )

    def z_copy(src, buf, ssem, rsem, target, slot):
        return pltpu.make_async_remote_copy(
            src_ref=src,
            dst_ref=buf.at[slot],
            send_sem=ssem.at[target],
            recv_sem=rsem.at[slot],
            device_id=(c, target),
            device_id_type=MESH,
        )

    def strip_copy(it, tc, tz, slot):
        return pltpu.make_async_remote_copy(
            src_ref=strip_out.at[it],
            dst_ref=strips.at[it, slot],
            send_sem=strip_s.at[it, tc * zs + tz],
            recv_sem=strip_r.at[it, slot],
            device_id=(tc, tz),
            device_id_type=MESH,
        )

    def new_copy(target, slot):
        return pltpu.make_async_remote_copy(
            src_ref=new_out,
            dst_ref=news.at[slot],
            send_sem=new_s.at[target],
            recv_sem=new_r.at[slot],
            device_id=(target, z),
            device_id_type=MESH,
        )

    def others(count, mine, body):
        def step(i, carry):
            body(wrap(mine + i, count))
            return carry

        lax.fori_loop(1, count, step, 0)

    def cell_moment(it, src):
        acc = jnp.zeros((cols, terms), jnp.float32)
        for p in range(patches):
            acc = acc + nt(nt(src[p], up[p]), su[p])
        mom_out[it, :, :] = jnp.zeros(mom_out.shape[1:], jnp.float32)
        mom_out[it, :, 0:terms] = acc

    def apply_operator(it):
        first = c * patches - patches
        if it == 0:

            def near_wait(p, carry):
                near_copy(p).wait()
                return carry

            lax.fori_loop(0, patches, near_wait, 0)
        source = rhs if it == 0 else own_dir
        for p in range(patches):
            own_img[it, p] = nt(source[p].astype(jnp.bfloat16), blocks[p, 0], None)
        halo_copy(it, own_dir, 0).wait_recv()
        halo_copy(it, own_dir, 1).wait_recv()
        for p in range(patches):
            acc = own_img[it, p]
            for j in range(1, neigh.shape[0]):
                spot = wrap(neigh[j, p] - first + total, total)
                spot = jnp.minimum(wrap(spot, total), 3 * patches - 1)
                acc = acc + nt(halo[it, spot].astype(jnp.bfloat16), blocks[p, j], None)
            own_img[it, p] = acc
        others(cells, c, lambda s: moment_copy(it, s, s).wait_recv())
        local = jnp.zeros((cols, terms), jnp.float32)
        for j in range(far.shape[1]):
            local = local + nt(moment[it, far[0, j]][:, 0:terms], tr[0, j])
        high, low = split(local)
        local = jnp.concatenate(
            [high.astype(jnp.float32), high.astype(jnp.float32), low.astype(jnp.float32)], axis=1
        ).astype(jnp.bfloat16)
        for p in range(patches):
            own_img[it, p] += jnp.dot(local, gcat[p], preferred_element_type=jnp.float32)

    def assemble(full, buf):
        for p in range(patches):
            for s in range(zs):
                full[p, s * cols : (s + 1) * cols, :] = buf[s, p]

    map_copies[5].wait()
    map_copies[0].wait()
    map_copies[1].wait()
    cell_moment(0, rhs)
    halo[0, pl.ds(patches, patches)] = rhs[...]
    gathered[z] = rhs[...]
    pl.semaphore_wait(barrier, devices - 1)
    halo_copy(0, rhs, 0).start()
    halo_copy(0, rhs, 1).start()
    others(cells, c, lambda t: moment_copy(0, t, c).start())
    others(zs, z, lambda t: z_copy(rhs, gathered, gat_s, gat_r, t, z).start())

    for copy in map_copies[2:5]:
        copy.wait()
    for p in range(patches):
        both = lax.dot_general(
            sd[p],
            dn[p],
            (((0,), (0,)), ((), ())),
            precision=HIGH,
            preferred_element_type=jnp.float32,
        )
        high, low = split(both)
        gcat[p, 0:terms, :] = high
        gcat[p, terms : 2 * terms, :] = low
        gcat[p, 2 * terms : 3 * terms, :] = high

    def combine_up():
        for p in range(patches):
            high, low = split(nn(su[p], up[p]))
            ucat[p, 0:terms, :] = high
            ucat[p, terms : 2 * terms, :] = low

    def later_moment(it, src):
        acc = jnp.zeros((2 * cols, 2 * terms), jnp.float32)
        for p in range(patches):
            high, low = split(src[p])
            x = jnp.concatenate([high.astype(jnp.float32), low.astype(jnp.float32)], axis=0)
            acc = acc + nt(x.astype(jnp.bfloat16), ucat[p], None)
        acc = acc[:, 0:terms] + acc[:, terms:]
        mom_out[it, :, :] = jnp.zeros(mom_out.shape[1:], jnp.float32)
        mom_out[it, :, 0:terms] = acc[0:cols] + acc[cols:]

    sel = (
        lax.broadcasted_iota(jnp.int32, (cols, total_cols), 1)
        == lax.broadcasted_iota(jnp.int32, (cols, total_cols), 0) + z * cols
    ).astype(jnp.float32)
    eye = (
        lax.broadcasted_iota(jnp.int32, (total_cols, total_cols), 1)
        == lax.broadcasted_iota(jnp.int32, (total_cols, total_cols), 0)
    ).astype(jnp.float32)

    def share_strips(it, direction, with_rr):
        acc = jnp.zeros(((2 if with_rr else 1) * cols, total_cols), jnp.float32)
        for p in range(patches):
            left = own_img[it, p]
            if with_rr:
                left = jnp.concatenate([left, rhs[p]], axis=0)
            acc = acc + nt(left, direction[p])
        if with_rr:
            acc = jnp.concatenate([acc[0:cols], acc[cols:]], axis=1)
        strip_out[it, :, 0 : acc.shape[1]] = acc
        strips[it, me] = strip_out[it]
        everyone(lambda tc, tz: strip_copy(it, tc, tz, me).start())

    def collect_strips(it):
        everyone(lambda tc, tz: strip_copy(it, tc, tz, tc * zs + tz).wait_recv())
        curve, cur = [], []
        for s in range(zs):
            acc = strips[it, s]
            for k in range(1, cells):
                acc = acc + strips[it, k * zs + s]
            curve.append(acc[:, 0:total_cols])
            cur.append(acc[:, total_cols : 2 * total_cols])
        curve = jnp.concatenate(curve, axis=0)
        cur = jnp.concatenate(cur, axis=0)
        return 0.5 * (curve + nt(eye, curve)), cur

    apply_operator(0)
    others(zs, z, lambda s: z_copy(rhs, gathered, gat_s, gat_r, s, s).wait_recv())
    assemble(full_r, gathered)
    share_strips(0, full_r, True)
    others(zs, z, lambda t: z_copy(own_img.at[0], images.at[0], img_s.at[0], img_r.at[0], t, z).start())
    images[0, z] = own_img[0]
    combine_up()
    curve, current = collect_strips(0)
    solved, inverse = eliminate(
        [jnp.concatenate([curve, current], axis=1), jnp.concatenate([current, eye], axis=1)]
    )
    alpha_t = nt(eye, solved[:, total_cols:])
    inverse = inverse[:, total_cols:]
    alpha_own = nt(sel, solved[:, total_cols:])
    others(
        zs,
        z,
        lambda s: z_copy(own_img.at[0], images.at[0], img_s.at[0], img_r.at[0], s, s).wait_recv(),
    )
    assemble(full_i, images.at[0])
    new = jnp.zeros((total_cols, total_cols), jnp.float32)
    for p in range(patches):
        r1 = full_r[p] - nn(alpha_t, full_i[p])
        full_d[p] = r1
        new = new + nt(r1, r1)
    new_out[:, 0:total_cols] = new
    news[c] = new_out[...]
    others(cells, c, lambda t: new_copy(t, c).start())
    for p in range(patches):
        own_res[p] = rhs[p] - nn(alpha_own, full_i[p])
        sol_out[p] = nn(alpha_own, full_r[p])
    others(cells, c, lambda s: new_copy(s, s).wait_recv())
    new = news[0]
    for k in range(1, cells):
        new = new + news[k]
    new = new[:, 0:total_cols]
    beta = nn(inverse, new)
    beta_t = nn(new, inverse)
    beta_own = nt(sel, beta)
    for p in range(patches):
        own_dir[p] = own_res[p] + nn(beta_own, full_r[p])
    halo_copy(1, own_dir, 0).start()
    halo_copy(1, own_dir, 1).start()
    later_moment(1, own_dir)
    others(cells, c, lambda t: moment_copy(1, t, c).start())
    halo[1, pl.ds(patches, patches)] = own_dir[...]
    for p in range(patches):
        full_d[p] += nn(beta_t, full_r[p])

    apply_operator(1)
    share_strips(1, full_d, False)
    others(zs, z, lambda t: z_copy(own_img.at[1], images.at[1], img_s.at[1], img_r.at[1], t, z).start())
    images[1, z] = own_img[1]
    curve, _ = collect_strips(1)
    (solved,) = eliminate([jnp.concatenate([curve, new], axis=1)])
    alpha_t = nt(eye, solved[:, total_cols:])
    alpha_own = nt(sel, solved[:, total_cols:])
    for p in range(patches):
        sol_out[p] += nn(alpha_own, full_d[p])
    others(
        zs,
        z,
        lambda s: z_copy(own_img.at[1], images.at[1], img_s.at[1], img_r.at[1], s, s).wait_recv(),
    )
    assemble(full_i, images.at[1])
    for p in range(patches):
        res_out[p] = own_res[p] - nn(alpha_own, full_i[p])

    for it in range(ITERS):
        halo_copy(it, own_dir, 0).wait_send()
        halo_copy(it, own_dir, 1).wait_send()
        others(cells, c, lambda t: moment_copy(it, t, c).wait_send())
        everyone(lambda tc, tz: strip_copy(it, tc, tz, me).wait_send())
        others(
            zs,
            z,
            lambda t: z_copy(
                own_img.at[it], images.at[it], img_s.at[it], img_r.at[it], t, z
            ).wait_send(),
        )
    others(zs, z, lambda t: z_copy(rhs, gathered, gat_s, gat_r, t, z).wait_send())
    others(cells, c, lambda t: new_copy(t, c).wait_send())


def on_device(cells, zs, *args):
    rhs, near, neigh, up, su, far, tr, sd, dn = args
    patches, cols, width = rhs.shape
    dn = jnp.swapaxes(dn, 1, 2)
    neigh = neigh.T
    full = cols * zs
    devices = cells * zs
    f32 = jnp.float32
    vmem = pl.BlockSpec(memory_space=pltpu.VMEM)
    smem = pl.BlockSpec(memory_space=pltpu.SMEM)
    hbm = pl.BlockSpec(memory_space=pltpu.HBM)
    dma = pltpu.SemaphoreType.DMA
    out = pl.pallas_call(
        functools.partial(kernel, cells, zs),
        out_shape=[jax.ShapeDtypeStruct(rhs.shape, f32)] * 2,
        in_specs=[hbm, hbm, smem, hbm, hbm, smem, hbm, hbm, hbm],
        out_specs=[vmem, vmem],
        scratch_shapes=[
            pltpu.VMEM(rhs.shape, f32),
            pltpu.VMEM(near.shape, near.dtype),
            pltpu.VMEM(up.shape, f32),
            pltpu.VMEM(su.shape, f32),
            pltpu.VMEM(tr.shape, f32),
            pltpu.VMEM(sd.shape, f32),
            pltpu.VMEM(dn.shape, f32),
            pltpu.VMEM((patches, 3 * su.shape[1], width), jnp.bfloat16),
            pltpu.VMEM((patches, 2 * su.shape[1], width), jnp.bfloat16),
            pltpu.VMEM((ITERS, 3 * patches, cols, width), f32),
            pltpu.VMEM((ITERS, cells, cols, 128), f32),
            pltpu.VMEM((ITERS, cols, 128), f32),
            pltpu.VMEM(rhs.shape, f32),
            pltpu.VMEM((ITERS,) + rhs.shape, f32),
            pltpu.VMEM(rhs.shape, f32),
            pltpu.VMEM((zs,) + rhs.shape, f32),
            pltpu.VMEM((ITERS, zs) + rhs.shape, f32),
            pltpu.VMEM((patches, full, width), f32),
            pltpu.VMEM((patches, full, width), f32),
            pltpu.VMEM((patches, full, width), f32),
            pltpu.VMEM((ITERS, cols, 128), f32),
            pltpu.VMEM((ITERS, devices, cols, 128), f32),
            pltpu.VMEM((full, 128), f32),
            pltpu.VMEM((cells, full, 128), f32),
            dma((patches,)),
            dma((6,)),
            dma((ITERS, 2)),
            dma((ITERS, 2)),
            dma((ITERS, cells)),
            dma((ITERS, cells)),
            dma((zs,)),
            dma((zs,)),
            dma((ITERS, zs)),
            dma((ITERS, zs)),
            dma((ITERS, devices)),
            dma((ITERS, devices)),
            dma((cells,)),
            dma((cells,)),
        ],
        compiler_params=pltpu.CompilerParams(
            collective_id=0, has_side_effects=True, vmem_limit_bytes=60 * 1024 * 1024
        ),
        name="block_cg",
    )(rhs, near, neigh, up, su, far, tr, sd, dn)
    return tuple(out)


def solution(mesh):
    cells = mesh.shape["patch"]
    zs = mesh.shape["rhs"]
    return jax.shard_map(
        functools.partial(on_device, cells, zs),
        mesh=mesh,
        in_specs=(
            P("patch", "rhs", None),
            P("patch", None, None, None),
            P("patch", None),
            P("patch", None, None),
            P("patch", None, None),
            P("patch", None),
            P("patch", None, None, None),
            P("patch", None, None),
            P("patch", None, None),
        ),
        out_specs=(P("patch", "rhs", None), P("patch", "rhs", None)),
        check_vma=False,
    )
```

profile of v0, /device:TPU:0, one launch (start us, length us, event | category | flops | bytes accessed | tf_op | source)
XLA Modules:
  0.0 47.8 jit_solution(9914071504025702654)
XLA Ops:
  0.6 44.3 %block_cg.1 = (f32[8,4,384]{2,1,0:T(4,128)}, f32[8,4,384]{2,1,0:T(4,128)}) custom-call(f32[8,4,384]{2,1,0:T(4,128)} %rhs_hbm.1, bf16[8,4,384,384]{3,2,1,0:T(8,128)(2,1)} %near_hbm.1, s32[4,8]{1,0:T(4,128)} %bitcast.3, f32[8,64,384]{2,1,0:T(8,128)} %up_hbm.1, f32[8,64,64]{2,1,0:T(8,128)} %su_hbm.1, s32[1,4]{1,0:T(1,128)} %far.1, f32[1,4,64,64]{3,2,1,0:T(8,128)} %tr_hbm.1, ...), custom_call_target="tpu_custom_call" | custom-call | tf_op jit(solution)/shard_map/block_cg/pallas_call | solution.py:423
  44.9 1.4 %copy.13 = f32[8,4,384]{2,1,0:T(4,128)} copy(f32[8,4,384]{2,1,0:T(4,128)} %get-tuple-element.4) | data formatting | bytes 98304
  46.3 1.4 %copy.14 = f32[8,4,384]{2,1,0:T(4,128)} copy(f32[8,4,384]{2,1,0:T(4,128)} %get-tuple-element.5) | data formatting | bytes 98304
where the time goes:
time: 48 us; the launch traced here: 47.8 us
  Pallas kernels  44.3 us (92%)
  local copies, waits for them, and re-layouts  2.85 us (6%)
  between operations  0.64 us (1%)
    pallas_call x1, Pallas kernels, on_device(): pl.pallas_call(functools.partial(kernel, cells, zs), out_shape=[jax.Shape...  44.3 us
    unnamed x2, local copies, waits for them, and re-layouts  2.85 us

commit v1 on v0

v1 whole, which is shorter than its diff:
```python
import functools

import jax
import jax.numpy as jnp
from jax import lax
from jax.experimental import pallas as pl
from jax.experimental.pallas import tpu as pltpu
from jax.sharding import PartitionSpec as P

MESH = pl.DeviceIdType.MESH
F32 = jnp.float32
BF16 = jnp.bfloat16


def nt(a, b):
    return lax.dot_general(a, b, (((1,), (1,)), ((), ())), preferred_element_type=F32)


def nn(a, b):
    return lax.dot_general(a, b, (((1,), (0,)), ((), ())), preferred_element_type=F32)


def wrap(i, n):
    return jnp.where(i >= n, i - n, i)


def split(x):
    high = x.astype(BF16)
    return high, (x - high.astype(F32)).astype(BF16)


def split3(x):
    high = x.astype(BF16)
    rest = x - high.astype(F32)
    middle = rest.astype(BF16)
    return high, middle, (rest - middle.astype(F32)).astype(BF16)


def rows_of(parts):
    return jnp.concatenate([x.astype(F32) for x in parts], axis=0).astype(BF16)


def exact(form, a, b):
    return lax.dot_general(
        a,
        b,
        (((1,), (0 if form is nn else 1,)), ((), ())),
        precision=lax.Precision.HIGHEST,
        preferred_element_type=F32,
    )


def product(form, a, b):
    ah, al = split(a)
    bh, bl = split(b)
    return form(ah, bh) + (form(ah, bl) + form(al, bh))


def eliminate(systems, n):
    state = [
        (a, [jnp.broadcast_to(a[:, first + j : first + j + 1], a.shape) for j in range(n)])
        for a, first in systems
    ]
    rows = lax.broadcasted_iota(jnp.int32, systems[0][0].shape, 0)
    for k in range(n):
        after = []
        for a, cols in state:
            pivot = cols[k]
            scale = 1.0 / pivot[k : k + 1, :]

            def update(x):
                row = x[k : k + 1, :] * scale
                return jnp.where(rows == k, row, x - pivot * row)

            after.append((update(a), [update(x) if j > k else x for j, x in enumerate(cols)]))
        state = after
    return [a for a, _ in state]


def kernel(
    cells,
    zs,
    chunks,
    rhs_hbm,
    near_hbm,
    neigh,
    up_hbm,
    su_hbm,
    far,
    tr_hbm,
    sd_hbm,
    dn_hbm,
    out,
    rhs,
    blocks,
    up,
    su,
    tr,
    sd,
    dn,
    ucat,
    gcat,
    halo0,
    halo1,
    mom0_out,
    mom0,
    momi_out,
    momi,
    loc_out,
    loc,
    gath_r,
    gath_i,
    base,
    img,
    part_r,
    part_s,
    first,
    second,
    gram_out,
    grams,
    turned,
    near_sem,
    map_sem,
    h0_s,
    h0_r,
    m0_s,
    m0_r,
    gr_s,
    gr_r,
    gi_s,
    gi_r,
    lo_s,
    lo_r,
    g_s,
    g_r,
    mi_s,
    mi_r,
    h1_s,
    h1_r,
):
    c = lax.axis_index("patch")
    z = lax.axis_index("rhs")
    patches, cols, width = rhs.shape
    terms = su.shape[1]
    k = cols * zs
    total = patches * cells
    lists = far.shape[1]
    near_count = neigh.shape[0]

    maps = [(rhs_hbm, rhs), (up_hbm, up), (su_hbm, su), (sd_hbm, sd), (dn_hbm, dn), (tr_hbm, tr)]
    map_copies = [
        pltpu.make_async_copy(src, dst, map_sem.at[i]) for i, (src, dst) in enumerate(maps)
    ]

    def near_copy(p, rest):
        part = pl.ds(1, near_count - 1) if rest else pl.ds(0, 1)
        return pltpu.make_async_copy(
            near_hbm.at[p, part], blocks.at[p, part], near_sem.at[p, 1 if rest else 0]
        )

    for copy in map_copies[:3]:
        copy.start()
    barrier = pltpu.get_barrier_semaphore()

    def cell_of(i):
        return wrap(c + i, cells)

    def row_of(i):
        return wrap(z + i, zs)

    for i in range(1, cells):
        pl.semaphore_signal(barrier, inc=1, device_id=(cell_of(i), z), device_id_type=MESH)
    for i in range(1, zs):
        pl.semaphore_signal(barrier, inc=1, device_id=(c, row_of(i)), device_id_type=MESH)
    for p in range(patches):
        near_copy(p, False).start()
    for copy in map_copies[3:]:
        copy.start()
    for p in range(patches):
        near_copy(p, True).start()

    def send(src, dst, ssem, rsem, device):
        return pltpu.make_async_remote_copy(
            src_ref=src,
            dst_ref=dst,
            send_sem=ssem,
            recv_sem=rsem,
            device_id=device,
            device_id_type=MESH,
        )

    def halo0_copy(side):
        return send(
            halo0.at[pl.ds(patches, patches)],
            halo0.at[pl.ds(0 if side == 0 else 2 * patches, patches)],
            h0_s.at[side],
            h0_r.at[side],
            (cell_of(1 if side == 0 else cells - 1), z),
        )

    step = patches // chunks

    def halo1_copy(side, i):
        return send(
            halo1.at[pl.ds(patches + i * step, step)],
            halo1.at[pl.ds((0 if side == 0 else 2 * patches) + i * step, step)],
            h1_s.at[side, i],
            h1_r.at[side, i],
            (cell_of(1 if side == 0 else cells - 1), z),
        )

    def plane_copy(src, buf, ssem, rsem, target, slot):
        return send(src, buf.at[slot], ssem.at[target], rsem.at[slot], (target, z))

    def z_copy(src, buf, ssem, rsem, target, slot):
        return send(src, buf.at[slot], ssem.at[target], rsem.at[slot], (c, target))

    def image_copy(p, target, slot):
        return send(
            gath_i.at[z, p], gath_i.at[slot, p], gi_s.at[target, p], gi_r.at[slot, p], (c, target)
        )

    def plane(body):
        for i in range(1, cells):
            body(cell_of(i))

    def line(body):
        for i in range(1, zs):
            body(row_of(i))

    def moment0_copy(target, slot):
        return plane_copy(mom0_out, mom0, m0_s, m0_r, target, slot)

    def momenti_copy(target, slot):
        return plane_copy(momi_out, momi, mi_s, mi_r, target, slot)

    def gram_copy(it, target, slot):
        return plane_copy(gram_out.at[it], grams.at[it], g_s.at[it], g_r.at[it], target, slot)

    def rhs_copy(target, slot):
        return z_copy(rhs, gath_r, gr_s, gr_r, target, slot)

    def local_copy(target, slot):
        return z_copy(loc_out, loc, lo_s, lo_r, target, slot)

    map_copies[0].wait()
    for p in range(patches):
        halo0[patches + p] = rhs[p].astype(BF16)
    pl.semaphore_wait(barrier, cells - 1 + zs - 1)
    halo0_copy(0).start()
    halo0_copy(1).start()
    line(lambda t: rhs_copy(t, z).start())

    map_copies[1].wait()
    map_copies[2].wait()
    acc = jnp.zeros((2 * cols, 2 * terms), F32)
    for p in range(patches):
        high, low = split(product(nn, su[p], up[p]))
        ucat[p, 0:terms, :] = high
        ucat[p, terms : 2 * terms, :] = low
        acc = acc + nt(rows_of(split(rhs[p])), ucat[p])
    acc = acc[0:cols] + acc[cols:]
    mom0_out[...] = jnp.concatenate([acc[:, 0:terms] + acc[:, terms:], jnp.zeros_like(acc[:, terms:])], axis=1)
    mom0[c] = mom0_out[...]
    plane(lambda t: moment0_copy(t, c).start())

    for p in range(patches):
        near_copy(p, False).wait()
        gath_i[z, p] = nt(halo0[patches + p], blocks[p, 0])
    for p in range(patches):
        gath_r[z, p] = rhs[p]

    for copy in map_copies[3:]:
        copy.wait()
    for p in range(patches):
        high, low = split(product(nn, sd[p].T, dn[p]))
        gcat[p, 0:terms, :] = high
        gcat[p, terms : 2 * terms, :] = low
    tall = jnp.concatenate([tr[0, j] for j in range(lists)], axis=1)

    def spot_of(p, j):
        spot = wrap(neigh[j, p] - (c * patches - patches) + total, total)
        return jnp.minimum(wrap(spot, total), 3 * patches - 1)

    halo0_copy(0).wait_recv()
    halo0_copy(1).wait_recv()
    for p in range(patches):
        near_copy(p, True).wait()
        acc = gath_i[z, p]
        for j in range(1, near_count):
            acc = acc + nt(halo0[spot_of(p, j)], blocks[p, j])
        gath_i[z, p] = acc
        line(lambda t, p=p: image_copy(p, t, z).start())

    def local_of(moments):
        wide = jnp.concatenate([moments[far[0, j]][:, 0:terms] for j in range(lists)], axis=1)
        return product(nt, wide, tall)

    plane(lambda s: moment0_copy(s, s).wait_recv())
    loc_out[...] = jnp.zeros(loc_out.shape, F32)
    loc_out[:, 0:terms] = local_of(mom0)
    loc[z] = loc_out[...]
    line(lambda t: local_copy(t, z).start())

    def far_of(local, p):
        high, low = split(local)
        both = jnp.concatenate(
            [jnp.concatenate([high, high], axis=1), jnp.concatenate([low, low], axis=1)], axis=0
        )
        both = nn(both, gcat[p])
        return both[0:k] + both[k:]

    line(lambda s: rhs_copy(s, s).wait_recv())
    for p in range(patches):
        for s in range(zs):
            img[p, s * cols : (s + 1) * cols, :] = gath_r[s, p]
        for i, x in enumerate(split3(img[p])):
            first[p, 2 * i * k : (2 * i + 1) * k, :] = x

    line(lambda s: local_copy(s, s).wait_recv())
    for s in range(zs):
        base[s * cols : (s + 1) * cols, :] = loc[s]
    local0 = base[:, 0:terms]
    acc1 = jnp.zeros((4 * k, 2 * k), F32)
    acc2 = jnp.zeros((4 * k, 2 * k), F32)
    for p in range(patches):
        whole = far_of(local0, p)
        line(lambda s, p=p: image_copy(p, s, s).wait_recv())
        for s in range(zs):
            img[p, s * cols : (s + 1) * cols, :] = gath_i[s, p]
        for i, x in enumerate(split3(img[p] + whole)):
            first[p, (2 * i + 1) * k : (2 * i + 2) * k, :] = x
        acc1 = acc1 + nt(first[p, 0 : 4 * k], first[p, 0 : 2 * k])
        acc2 = acc2 + nt(first[p, 0 : 4 * k], first[p, 2 * k : 4 * k])
    gram = acc1[0 : 2 * k] + (acc1[2 * k :] + acc2[0 : 2 * k] + acc2[2 * k :])
    top, low = gram[0:k], gram[k:]
    gram_out[0] = jnp.concatenate(
        [
            0.5 * (top[:, k:] + low[:, 0:k]),
            top[:, 0:k],
            low,
            top,
            jnp.zeros((k, 128 - 6 * k), F32),
        ],
        axis=1,
    )
    grams[0, c] = gram_out[0]
    plane(lambda t: gram_copy(0, t, c).start())

    acc = jnp.zeros((2 * k, 2 * terms), F32)
    for p in range(patches):
        acc = acc + nt(
            jnp.concatenate([first[p, k : 2 * k], first[p, 3 * k : 4 * k]], axis=0), ucat[p]
        )
    acc = acc[0:k] + acc[k:]
    momi_out[...] = jnp.concatenate([acc[:, 0:terms] + acc[:, terms:], jnp.zeros_like(acc[:, terms:])], axis=1)
    momi[c] = momi_out[...]
    plane(lambda t: momenti_copy(t, c).start())

    def collect(it):
        plane(lambda s: gram_copy(it, s, s).wait_recv())
        parts = [grams[it, i] for i in range(cells)]
        while len(parts) > 1:
            parts = [
                parts[i] + parts[i + 1] if i + 1 < len(parts) else parts[i]
                for i in range(0, len(parts), 2)
            ]
        return parts[0]

    eye = (
        lax.broadcasted_iota(jnp.int32, (k, k), 1) == lax.broadcasted_iota(jnp.int32, (k, k), 0)
    ).astype(F32)
    got = collect(0)
    one, two = eliminate([(got, 0), (got, 4 * k)], k)
    one_t, two_t = one.T, two.T
    alpha_t = one_t[k : 2 * k]
    beta1_t = (
        2.0 * eye
        - one_t[2 * k : 3 * k]
        + exact(nn, alpha_t, one_t[3 * k : 4 * k] - two_t[5 * k : 6 * k])
    )

    def doubled(x):
        high, low = split(x)
        high, low = high.astype(F32), low.astype(F32)
        return jnp.concatenate(
            [jnp.concatenate([high, high], axis=1), jnp.concatenate([low, low], axis=1)], axis=0
        ).astype(BF16)

    mixing = jnp.concatenate(
        [
            jnp.concatenate([x.astype(F32)] * 3, axis=1)
            for x in split3(jnp.concatenate([beta1_t, -alpha_t], axis=1))
        ],
        axis=0,
    ).astype(BF16)
    for p in range(patches):
        both = nn(mixing, first[p])
        high, low = split(both[0:k] + (both[k : 2 * k] + both[2 * k :]))
        halo1[patches + p] = high
        second[p, 0:k, :] = high
        second[p, k : 2 * k, :] = low
        if (p + 1) % step == 0:
            halo1_copy(0, p // step).start()
            halo1_copy(1, p // step).start()

    plane(lambda s: momenti_copy(s, s).wait_recv())
    local1 = product(nn, beta1_t, local0) - product(nn, alpha_t, local_of(momi))
    for p in range(patches):
        img[p] = nt(halo1[patches + p], blocks[p, 0]) + far_of(local1, p)
    mixed = exact(nt, got[:, 5 * k : 6 * k], alpha_t)
    new = (
        got[:, k : 2 * k]
        - mixed
        - mixed.T
        + exact(nn, alpha_t, exact(nt, got[:, 3 * k : 4 * k], alpha_t))
    )
    base[...] = jnp.zeros(base.shape, F32)
    base[:, k : 2 * k] = new
    right = base[...]
    turned[...] = one_t
    own = turned[pl.ds(k + z * cols, cols), :]
    high, low = [x.astype(F32) for x in split(own)]
    none = jnp.zeros_like(own)
    out_mix = jnp.concatenate(
        [
            jnp.concatenate([high, none, high, none], axis=1),
            jnp.concatenate([low, none, low, none], axis=1),
            jnp.concatenate([none, high, none, high], axis=1),
            jnp.concatenate([none, low, none, low], axis=1),
        ],
        axis=0,
    ).astype(BF16)
    for p in range(patches):
        both = nn(out_mix, first[p, 0 : 4 * k])
        part_s[p] = both[0:cols] + both[cols : 2 * cols]
        part_r[p] = rhs[p] - (both[2 * cols : 3 * cols] + both[3 * cols :])

    for i in range(chunks):
        halo1_copy(0, i).wait_recv()
        halo1_copy(1, i).wait_recv()
    acc1 = jnp.zeros((2 * k, k), F32)
    acc2 = jnp.zeros((k, k), F32)
    for p in range(patches):
        acc = img[p]
        for j in range(1, near_count):
            acc = acc + nt(halo1[spot_of(p, j)], blocks[p, j])
        high, low = split(acc)
        second[p, 2 * k : 3 * k, :] = high
        second[p, 3 * k : 4 * k, :] = low
        acc1 = acc1 + nt(second[p, 0 : 2 * k], high)
        acc2 = acc2 + nt(second[p, 0:k], low)
    curve = acc1[0:k] + acc1[k:] + acc2
    gram_out[1] = jnp.concatenate(
        [0.5 * (curve + curve.T), jnp.zeros((k, 128 - k), F32)], axis=1
    )
    grams[1, c] = gram_out[1]
    plane(lambda t: gram_copy(1, t, c).start())
    (last,) = eliminate([(collect(1) + right, 0)], k)
    turned[...] = last.T
    out_mix = doubled(turned[pl.ds(k + z * cols, cols), :])
    for p in range(patches):
        both = nn(out_mix, second[p, 0 : 2 * k])
        out[p, 0:cols, :] = part_s[p] + (both[0:cols] + both[cols:])
        both = nn(out_mix, second[p, 2 * k : 4 * k])
        out[p, cols : 2 * cols, :] = part_r[p] - (both[0:cols] + both[cols:])

    for side in range(2):
        halo0_copy(side).wait_send()
        for i in range(chunks):
            halo1_copy(side, i).wait_send()
    line(lambda t: rhs_copy(t, z).wait_send())
    line(lambda t: local_copy(t, z).wait_send())
    for p in range(patches):
        line(lambda t, p=p: image_copy(p, t, z).wait_send())
    plane(lambda t: moment0_copy(t, c).wait_send())
    plane(lambda t: momenti_copy(t, c).wait_send())
    for it in range(2):
        plane(lambda t, it=it: gram_copy(it, t, c).wait_send())


def on_device(cells, zs, *args):
    rhs, near, neigh, up, su, far, tr, sd, dn = args
    patches, cols, width = rhs.shape
    terms = su.shape[1]
    dn = jnp.swapaxes(dn, 1, 2)
    neigh = neigh.T
    k = cols * zs
    chunks = 4 if patches % 4 == 0 else 1
    vmem = pl.BlockSpec(memory_space=pltpu.VMEM)
    smem = pl.BlockSpec(memory_space=pltpu.SMEM)
    hbm = pl.BlockSpec(memory_space=pltpu.HBM)
    dma = pltpu.SemaphoreType.DMA
    out = pl.pallas_call(
        functools.partial(kernel, cells, zs, chunks),
        out_shape=jax.ShapeDtypeStruct((patches, 2 * cols, width), F32),
        in_specs=[hbm, hbm, smem, hbm, hbm, smem, hbm, hbm, hbm],
        out_specs=vmem,
        scratch_shapes=[
            pltpu.VMEM(rhs.shape, F32),
            pltpu.VMEM(near.shape, near.dtype),
            pltpu.VMEM(up.shape, F32),
            pltpu.VMEM(su.shape, F32),
            pltpu.VMEM(tr.shape, F32),
            pltpu.VMEM(sd.shape, F32),
            pltpu.VMEM(dn.shape, F32),
            pltpu.VMEM((patches, 2 * terms, width), BF16),
            pltpu.VMEM((patches, 2 * terms, width), BF16),
            pltpu.VMEM((3 * patches, cols, width), BF16),
            pltpu.VMEM((3 * patches, k, width), BF16),
            pltpu.VMEM((cols, 128), F32),
            pltpu.VMEM((cells, cols, 128), F32),
            pltpu.VMEM((k, 128), F32),
            pltpu.VMEM((cells, k, 128), F32),
            pltpu.VMEM((cols, 128), F32),
            pltpu.VMEM((zs, cols, 128), F32),
            pltpu.VMEM((zs,) + rhs.shape, F32),
            pltpu.VMEM((zs,) + rhs.shape, F32),
            pltpu.VMEM((k, 128), F32),
            pltpu.VMEM((patches, k, width), F32),
            pltpu.VMEM(rhs.shape, F32),
            pltpu.VMEM(rhs.shape, F32),
            pltpu.VMEM((patches, 6 * k, width), BF16),
            pltpu.VMEM((patches, 4 * k, width), BF16),
            pltpu.VMEM((2, k, 128), F32),
            pltpu.VMEM((2, cells, k, 128), F32),
            pltpu.VMEM((128, k), F32),
            dma((patches, 2)),
            dma((6,)),
            dma((2,)),
            dma((2,)),
            dma((cells,)),
            dma((cells,)),
            dma((zs,)),
            dma((zs,)),
            dma((zs, patches)),
            dma((zs, patches)),
            dma((zs,)),
            dma((zs,)),
            dma((2, cells)),
            dma((2, cells)),
            dma((cells,)),
            dma((cells,)),
            dma((2, chunks)),
            dma((2, chunks)),
        ],
        compiler_params=pltpu.CompilerParams(
            collective_id=0, has_side_effects=True, vmem_limit_bytes=60 * 1024 * 1024
        ),
        name="block_cg",
    )(rhs, near, neigh, up, su, far, tr, sd, dn)
    return out[:, 0:cols], out[:, cols:]


def solution(mesh):
    cells = mesh.shape["patch"]
    zs = mesh.shape["rhs"]
    return jax.shard_map(
        functools.partial(on_device, cells, zs),
        mesh=mesh,
        in_specs=(
            P("patch", "rhs", None),
            P("patch", None, None, None),
            P("patch", None),
            P("patch", None, None),
            P("patch", None, None),
            P("patch", None),
            P("patch", None, None, None),
            P("patch", None, None),
            P("patch", None, None),
        ),
        out_specs=(P("patch", "rhs", None), P("patch", "rhs", None)),
        check_vma=False,
    )
```

time: 48 us -> 38.3 us (0.80)
  Pallas kernels: 44.3 us -> 35.9 us
  local copies, waits for them, and re-layouts: 2.85 us -> 1.62 us
    pallas_call x1, Pallas kernels: 44.3 us -> 35.9 us  [on_device(): pl.pallas_call(functools.partial(kernel, cells, zs, chunks), out_shape=ja...]
    unnamed x2 -> x0, local copies, waits for them, and re-layouts: 2.85 us -> none
    slice x0 -> x1, local copies, waits for them, and re-layouts: none -> 1.62 us  [on_device(): return (out[:, 0:cols], out[:, cols:])]
where the time goes in v1:
time: 38.3 us; the launch traced here: 38.1 us
  Pallas kernels  35.9 us (94%)
  local copies, waits for them, and re-layouts  1.62 us (4%)
  between operations  0.64 us (2%)
    pallas_call x1, Pallas kernels, on_device(): pl.pallas_call(functools.partial(kernel, cells, zs, chunks), out_shape=ja...  35.9 us
    slice x1, local copies, waits for them, and re-layouts, on_device(): return (out[:, 0:cols], out[:, cols:])  1.62 us

profile of v1, /device:TPU:0, one launch (start us, length us, event | category | flops | bytes accessed | tf_op | source)
XLA Modules:
  0.0 38.1 jit_solution(7389184446104985273)
XLA Ops:
  0.6 35.9 %block_cg.1 = f32[8,8,384]{2,1,0:T(8,128)} custom-call(f32[8,4,384]{2,1,0:T(4,128)} %rhs_hbm.1, bf16[8,4,384,384]{3,2,1,0:T(8,128)(2,1)} %near_hbm.1, s32[4,8]{1,0:T(4,128)} %bitcast.3, f32[8,64,384]{2,1,0:T(8,128)} %up_hbm.1, f32[8,64,64]{2,1,0:T(8,128)} %su_hbm.1, s32[1,4]{1,0:T(1,128)} %far.1, f32[1,4,64,64]{3,2,1,0:T(8,128)} %tr_hbm.1, ...), custom_call_target="tpu_custom_call" | custom-call | tf_op jit(solution)/shard_map/block_cg/pallas_call | solution.py:494
  36.5 1.6 %fusion = (f32[8,4,384]{2,1,0:T(4,128)}, f32[8,4,384]{2,1,0:T(4,128)}) fusion(f32[8,8,384]{2,1,0:T(8,128)} %block_cg.1), kind=kLoop, calls=%fused_computation | loop fusion | bytes 196608 | tf_op jit(solution)/shard_map/slice | solution.py:552

commit v2 on v1

--- a/solution.py
+++ b/solution.py
@@ -137,6 +137,8 @@
     mi_r,
     h1_s,
     h1_r,
+    in_above,
+    in_below,
 ):
     c = lax.axis_index("patch")
     z = lax.axis_index("rhs")
@@ -170,14 +172,30 @@
 
     for i in range(1, cells):
         pl.semaphore_signal(barrier, inc=1, device_id=(cell_of(i), z), device_id_type=MESH)
-    for i in range(1, zs):
-        pl.semaphore_signal(barrier, inc=1, device_id=(c, row_of(i)), device_id_type=MESH)
-    for p in range(patches):
-        near_copy(p, False).start()
-    for copy in map_copies[3:]:
-        copy.start()
-    for p in range(patches):
-        near_copy(p, True).start()
+
+    def below(i, body):
+        pl.when(z >= i)(body)
+
+    def above(i, body):
+        pl.when(z < zs - i)(body)
+
+    below(1, lambda: pl.semaphore_signal(barrier, inc=1, device_id=(c, z - 1), device_id_type=MESH))
+    above(1, lambda: pl.semaphore_signal(barrier, inc=1, device_id=(c, z + 1), device_id_type=MESH))
+
+    def tell(i):
+        def down():
+            pl.semaphore_signal(in_above.at[i - 1], inc=1, device_id=(c, z - 1), device_id_type=MESH)
+
+        def up():
+            pl.semaphore_signal(in_below.at[i - 1], inc=1, device_id=(c, z + 1), device_id_type=MESH)
+
+        pl.when((z >= 1) & (z < zs - i))(down)
+        pl.when((z >= i) & (z < zs - 1))(up)
+
+    def hear(i):
+        above(i + 1, lambda: pl.semaphore_wait(in_above.at[i - 1], 1))
+        below(i + 1, lambda: pl.semaphore_wait(in_below.at[i - 1], 1))
+
 
     def send(src, dst, ssem, rsem, device):
         return pltpu.make_async_remote_copy(
@@ -215,9 +233,18 @@
     def z_copy(src, buf, ssem, rsem, target, slot):
         return send(src, buf.at[slot], ssem.at[target], rsem.at[slot], (c, target))
 
-    def image_copy(p, target, slot):
+    pieces = 4 if patches % 4 == 0 else 1
+    piece = patches // pieces
+    group = 2 if pieces > 1 else 1
+
+    def image_copy(i, target, slot):
+        part = pl.ds(i * piece, piece)
         return send(
-            gath_i.at[z, p], gath_i.at[slot, p], gi_s.at[target, p], gi_r.at[slot, p], (c, target)
+            gath_i.at[z, part],
+            gath_i.at[slot, part],
+            gi_s.at[target, i],
+            gi_r.at[slot, i],
+            (c, target),
         )
 
     def plane(body):
@@ -245,14 +272,29 @@
 
     map_copies[0].wait()
     for p in range(patches):
+        near_copy(p, False).start()
+    for p in range(patches):
+        near_copy(p, True).start()
+    for copy in map_copies[3:]:
+        copy.start()
+    for p in range(patches):
         halo0[patches + p] = rhs[p].astype(BF16)
-    pl.semaphore_wait(barrier, cells - 1 + zs - 1)
+        gath_r[z, p] = rhs[p]
+    map_copies[1].wait()
+    map_copies[2].wait()
+
+    pl.semaphore_wait(barrier, cells - 1 + jnp.where(z > 0, 1, 0) + jnp.where(z < zs - 1, 1, 0))
     halo0_copy(0).start()
     halo0_copy(1).start()
-    line(lambda t: rhs_copy(t, z).start())
-
-    map_copies[1].wait()
-    map_copies[2].wait()
+
+    def share(i):
+        below(i, lambda: rhs_copy(z - i, z).start())
+        above(i, lambda: rhs_copy(z + i, z).start())
+
+    if zs > 2:
+        tell(1)
+    share(1)
+
     acc = jnp.zeros((2 * cols, 2 * terms), F32)
     for p in range(patches):
         high, low = split(product(nn, su[p], up[p]))
@@ -260,47 +302,55 @@
         ucat[p, terms : 2 * terms, :] = low
         acc = acc + nt(rows_of(split(rhs[p])), ucat[p])
     acc = acc[0:cols] + acc[cols:]
-    mom0_out[...] = jnp.concatenate([acc[:, 0:terms] + acc[:, terms:], jnp.zeros_like(acc[:, terms:])], axis=1)
+    acc = acc[:, 0:terms] + acc[:, terms:]
+    mom0_out[...] = jnp.concatenate([acc, jnp.zeros((cols, 128 - terms), F32)], axis=1)
     mom0[c] = mom0_out[...]
     plane(lambda t: moment0_copy(t, c).start())
+    if zs > 2:
+        hear(1)
+        if zs > 3:
+            tell(2)
+        share(2)
 
     for p in range(patches):
         near_copy(p, False).wait()
+    for p in range(patches):
         gath_i[z, p] = nt(halo0[patches + p], blocks[p, 0])
-    for p in range(patches):
-        gath_r[z, p] = rhs[p]
-
-    for copy in map_copies[3:]:
-        copy.wait()
-    for p in range(patches):
-        high, low = split(product(nn, sd[p].T, dn[p]))
-        gcat[p, 0:terms, :] = high
-        gcat[p, terms : 2 * terms, :] = low
+    for i in range(2, zs - 1):
+        hear(i)
+        if i < zs - 2:
+            tell(i + 1)
+        share(i + 1)
+
+    map_copies[5].wait()
     tall = jnp.concatenate([tr[0, j] for j in range(lists)], axis=1)
 
     def spot_of(p, j):
         spot = wrap(neigh[j, p] - (c * patches - patches) + total, total)
         return jnp.minimum(wrap(spot, total), 3 * patches - 1)
 
-    halo0_copy(0).wait_recv()
-    halo0_copy(1).wait_recv()
-    for p in range(patches):
-        near_copy(p, True).wait()
-        acc = gath_i[z, p]
-        for j in range(1, near_count):
-            acc = acc + nt(halo0[spot_of(p, j)], blocks[p, j])
-        gath_i[z, p] = acc
-        line(lambda t, p=p: image_copy(p, t, z).start())
-
     def local_of(moments):
         wide = jnp.concatenate([moments[far[0, j]][:, 0:terms] for j in range(lists)], axis=1)
         return product(nt, wide, tall)
 
-    plane(lambda s: moment0_copy(s, s).wait_recv())
-    loc_out[...] = jnp.zeros(loc_out.shape, F32)
-    loc_out[:, 0:terms] = local_of(mom0)
-    loc[z] = loc_out[...]
-    line(lambda t: local_copy(t, z).start())
+    for p in range(patches):
+        near_copy(p, True).wait()
+    halo0_copy(0).wait_recv()
+    halo0_copy(1).wait_recv()
+    for i in range(pieces):
+        for p in range(i * piece, (i + 1) * piece):
+            acc = gath_i[z, p]
+            for j in range(1, near_count):
+                acc = acc + nt(halo0[spot_of(p, j)], blocks[p, j])
+            gath_i[z, p] = acc
+        line(lambda t, i=i: image_copy(i, t, z).start())
+        if i == pieces // 2 - 1 or pieces == 1:
+            plane(lambda s: moment0_copy(s, s).wait_recv())
+            loc_out[...] = jnp.concatenate(
+                [local_of(mom0), jnp.zeros((cols, 128 - terms), F32)], axis=1
+            )
+            loc[z] = loc_out[...]
+            line(lambda t: local_copy(t, z).start())
 
     def far_of(local, p):
         high, low = split(local)
@@ -310,28 +360,39 @@
         both = nn(both, gcat[p])
         return both[0:k] + both[k:]
 
+    for copy in map_copies[3:5]:
+        copy.wait()
+    for p in range(patches):
+        high, low = split(product(nn, sd[p].T, dn[p]))
+        gcat[p, 0:terms, :] = high
+        gcat[p, terms : 2 * terms, :] = low
+
     line(lambda s: rhs_copy(s, s).wait_recv())
     for p in range(patches):
-        for s in range(zs):
-            img[p, s * cols : (s + 1) * cols, :] = gath_r[s, p]
-        for i, x in enumerate(split3(img[p])):
+        for i, x in enumerate(split3(jnp.concatenate([gath_r[s, p] for s in range(zs)], axis=0))):
             first[p, 2 * i * k : (2 * i + 1) * k, :] = x
 
     line(lambda s: local_copy(s, s).wait_recv())
-    for s in range(zs):
-        base[s * cols : (s + 1) * cols, :] = loc[s]
-    local0 = base[:, 0:terms]
+    local0 = jnp.concatenate([loc[s] for s in range(zs)], axis=0)[:, 0:terms]
+    for p in range(patches):
+        img[p] = far_of(local0, p)
     acc1 = jnp.zeros((4 * k, 2 * k), F32)
     acc2 = jnp.zeros((4 * k, 2 * k), F32)
-    for p in range(patches):
-        whole = far_of(local0, p)
-        line(lambda s, p=p: image_copy(p, s, s).wait_recv())
-        for s in range(zs):
-            img[p, s * cols : (s + 1) * cols, :] = gath_i[s, p]
-        for i, x in enumerate(split3(img[p] + whole)):
-            first[p, (2 * i + 1) * k : (2 * i + 2) * k, :] = x
-        acc1 = acc1 + nt(first[p, 0 : 4 * k], first[p, 0 : 2 * k])
-        acc2 = acc2 + nt(first[p, 0 : 4 * k], first[p, 2 * k : 4 * k])
+    for i in range(pieces):
+        if i % group == 0:
+            for j in range(i, i + group):
+                line(lambda s, j=j: image_copy(j, s, s).wait_recv())
+        for p in range(i * piece, (i + 1) * piece):
+            whole = jnp.concatenate([gath_i[s, p] for s in range(zs)], axis=0) + img[p]
+            high, middle, low = split3(whole)
+            first[p, k : 2 * k, :] = high
+            first[p, 3 * k : 4 * k, :] = middle
+            first[p, 5 * k : 6 * k, :] = low
+            one = jnp.concatenate([first[p, 0:k], high], axis=0)
+            two = jnp.concatenate([first[p, 2 * k : 3 * k], middle], axis=0)
+            both = jnp.concatenate([one, two], axis=0)
+            acc1 = acc1 + nt(both, one)
+            acc2 = acc2 + nt(both, two)
     gram = acc1[0 : 2 * k] + (acc1[2 * k :] + acc2[0 : 2 * k] + acc2[2 * k :])
     top, low = gram[0:k], gram[k:]
     gram_out[0] = jnp.concatenate(
@@ -353,7 +414,8 @@
             jnp.concatenate([first[p, k : 2 * k], first[p, 3 * k : 4 * k]], axis=0), ucat[p]
         )
     acc = acc[0:k] + acc[k:]
-    momi_out[...] = jnp.concatenate([acc[:, 0:terms] + acc[:, terms:], jnp.zeros_like(acc[:, terms:])], axis=1)
+    acc = acc[:, 0:terms] + acc[:, terms:]
+    momi_out[...] = jnp.concatenate([acc, jnp.zeros((k, 128 - terms), F32)], axis=1)
     momi[c] = momi_out[...]
     plane(lambda t: momenti_copy(t, c).start())
 
@@ -471,8 +533,8 @@
             halo1_copy(side, i).wait_send()
     line(lambda t: rhs_copy(t, z).wait_send())
     line(lambda t: local_copy(t, z).wait_send())
-    for p in range(patches):
-        line(lambda t, p=p: image_copy(p, t, z).wait_send())
+    for i in range(pieces):
+        line(lambda t, i=i: image_copy(i, t, z).wait_send())
     plane(lambda t: moment0_copy(t, c).wait_send())
     plane(lambda t: momenti_copy(t, c).wait_send())
     for it in range(2):
@@ -493,7 +555,7 @@
     dma = pltpu.SemaphoreType.DMA
     out = pl.pallas_call(
         functools.partial(kernel, cells, zs, chunks),
-        out_shape=jax.ShapeDtypeStruct((patches, 2 * cols, width), F32),
+        out_shape=pltpu.VMEM((patches, 2 * cols, width), F32),
         in_specs=[hbm, hbm, smem, hbm, hbm, smem, hbm, hbm, hbm],
         out_specs=vmem,
         scratch_shapes=[
@@ -543,6 +605,8 @@
             dma((cells,)),
             dma((2, chunks)),
             dma((2, chunks)),
+            pltpu.SemaphoreType.REGULAR((zs,)),
+            pltpu.SemaphoreType.REGULAR((zs,)),
         ],
         compiler_params=pltpu.CompilerParams(
             collective_id=0, has_side_effects=True, vmem_limit_bytes=60 * 1024 * 1024

time: 38.3 us -> 35.3 us (0.922)
  Pallas kernels: 35.9 us -> 33.8 us
  local copies, waits for them, and re-layouts: 1.62 us -> 0.65 us
    pallas_call x1, Pallas kernels: 35.9 us -> 33.8 us  [on_device(): pl.pallas_call(functools.partial(kernel, cells, zs, chunks), out_shape=pl...]
    slice x1, local copies, waits for them, and re-layouts: 1.62 us -> 0.65 us  [on_device(): return (out[:, 0:cols], out[:, cols:])]
where the time goes in v2:
time: 35.3 us; the launch traced here: 35.1 us
  Pallas kernels  33.8 us (96%)
  local copies, waits for them, and re-layouts  0.65 us (2%)
  between operations  0.64 us (2%)
    pallas_call x1, Pallas kernels, on_device(): pl.pallas_call(functools.partial(kernel, cells, zs, chunks), out_shape=pl...  33.8 us

profile of v2, /device:TPU:0, one launch (start us, length us, event | category | flops | bytes accessed | tf_op | source)
XLA Modules:
  0.0 35.1 jit_solution(17796753859667412361)
XLA Ops:
  0.6 33.8 %block_cg.1 = f32[8,8,384]{2,1,0:T(8,128)S(1)} custom-call(f32[8,4,384]{2,1,0:T(4,128)} %rhs_hbm.1, bf16[8,4,384,384]{3,2,1,0:T(8,128)(2,1)} %near_hbm.1, s32[4,8]{1,0:T(4,128)} %bitcast.3, f32[8,64,384]{2,1,0:T(8,128)} %up_hbm.1, f32[8,64,64]{2,1,0:T(8,128)} %su_hbm.1, s32[1,4]{1,0:T(1,128)} %far.1, f32[1,4,64,64]{3,2,1,0:T(8,128)} %tr_hbm.1, ...), custom_call_target="tpu_custom_call" | custom-call | tf_op jit(solution)/shard_map/block_cg/pallas_call | solution.py:556
  34.5 0.7 %fusion = (f32[8,4,384]{2,1,0:T(4,128)}, f32[8,4,384]{2,1,0:T(4,128)}) fusion(f32[8,8,384]{2,1,0:T(8,128)S(1)} %block_cg.1), kind=kLoop, calls=%fused_computation | loop fusion | bytes 196608 | tf_op jit(solution)/shard_map/slice | solution.py:616

commit v3 on v1

--- a/solution.py
+++ b/solution.py
@@ -100,6 +100,7 @@
     dn,
     ucat,
     gcat,
+    pieces,
     halo0,
     halo1,
     mom0_out,
@@ -109,7 +110,6 @@
     loc_out,
     loc,
     gath_r,
-    gath_i,
     base,
     img,
     part_r,
@@ -127,8 +127,8 @@
     m0_r,
     gr_s,
     gr_r,
-    gi_s,
-    gi_r,
+    pz_s,
+    pz_r,
     lo_s,
     lo_r,
     g_s,
@@ -170,14 +170,15 @@
 
     for i in range(1, cells):
         pl.semaphore_signal(barrier, inc=1, device_id=(cell_of(i), z), device_id_type=MESH)
+
     for i in range(1, zs):
         pl.semaphore_signal(barrier, inc=1, device_id=(c, row_of(i)), device_id_type=MESH)
-    for p in range(patches):
-        near_copy(p, False).start()
-    for copy in map_copies[3:]:
-        copy.start()
-    for p in range(patches):
-        near_copy(p, True).start()
+
+    def below(i, body):
+        pl.when(z >= i)(body)
+
+    def above(i, body):
+        pl.when(z < zs - i)(body)
 
     def send(src, dst, ssem, rsem, device):
         return pltpu.make_async_remote_copy(
@@ -189,12 +190,17 @@
             device_id_type=MESH,
         )
 
-    def halo0_copy(side):
+    def piece_copy(target, slot):
         return send(
-            halo0.at[pl.ds(patches, patches)],
-            halo0.at[pl.ds(0 if side == 0 else 2 * patches, patches)],
-            h0_s.at[side],
-            h0_r.at[side],
+            pieces.at[1, z], pieces.at[1, slot], pz_s.at[target], pz_r.at[slot], (c, target)
+        )
+
+    def relay_copy(side, s):
+        return send(
+            pieces.at[1, s],
+            pieces.at[2 * side, s],
+            h0_s.at[side, s],
+            h0_r.at[side, s],
             (cell_of(1 if side == 0 else cells - 1), z),
         )
 
@@ -215,11 +221,6 @@
     def z_copy(src, buf, ssem, rsem, target, slot):
         return send(src, buf.at[slot], ssem.at[target], rsem.at[slot], (c, target))
 
-    def image_copy(p, target, slot):
-        return send(
-            gath_i.at[z, p], gath_i.at[slot, p], gi_s.at[target, p], gi_r.at[slot, p], (c, target)
-        )
-
     def plane(body):
         for i in range(1, cells):
             body(cell_of(i))
@@ -245,11 +246,21 @@
 
     map_copies[0].wait()
     for p in range(patches):
-        halo0[patches + p] = rhs[p].astype(BF16)
+        near_copy(p, False).start()
+    for p in range(patches):
+        near_copy(p, True).start()
+    for copy in map_copies[3:]:
+        copy.start()
+    for p in range(patches):
+        pieces[1, z, p] = rhs[p].astype(BF16)
+        gath_r[z, p] = rhs[p]
+
     pl.semaphore_wait(barrier, cells - 1 + zs - 1)
-    halo0_copy(0).start()
-    halo0_copy(1).start()
-    line(lambda t: rhs_copy(t, z).start())
+    for i in range(1, zs):
+        below(i, lambda: piece_copy(z - i, z).start())
+        above(i, lambda: piece_copy(z + i, z).start())
+    relay_copy(0, z).start()
+    relay_copy(1, z).start()
 
     map_copies[1].wait()
     map_copies[2].wait()
@@ -260,47 +271,50 @@
         ucat[p, terms : 2 * terms, :] = low
         acc = acc + nt(rows_of(split(rhs[p])), ucat[p])
     acc = acc[0:cols] + acc[cols:]
-    mom0_out[...] = jnp.concatenate([acc[:, 0:terms] + acc[:, terms:], jnp.zeros_like(acc[:, terms:])], axis=1)
+    acc = acc[:, 0:terms] + acc[:, terms:]
+    mom0_out[...] = jnp.concatenate([acc, jnp.zeros((cols, 128 - terms), F32)], axis=1)
     mom0[c] = mom0_out[...]
     plane(lambda t: moment0_copy(t, c).start())
 
+    def pass_on(s):
+        piece_copy(s, s).wait_recv()
+        relay_copy(0, s).start()
+        relay_copy(1, s).start()
+
+    for i in range(1, zs):
+        below(i, lambda: pass_on(z - i))
+        above(i, lambda: pass_on(z + i))
+        if i == 1:
+            line(lambda t: rhs_copy(t, z).start())
+
+    map_copies[5].wait()
+    tall = jnp.concatenate([tr[0, j] for j in range(lists)], axis=1)
+
+    def local_of(moments):
+        wide = jnp.concatenate([moments[far[0, j]][:, 0:terms] for j in range(lists)], axis=1)
+        return product(nt, wide, tall)
+
+    plane(lambda s: moment0_copy(s, s).wait_recv())
+    loc_out[...] = jnp.concatenate([local_of(mom0), jnp.zeros((cols, 128 - terms), F32)], axis=1)
+    loc[z] = loc_out[...]
+    line(lambda t: local_copy(t, z).start())
+
+    def join(side):
+        for p in range(patches):
+            halo0[side * patches + p] = rows_of([pieces[side, s, p] for s in range(zs)])
+
+    join(1)
     for p in range(patches):
         near_copy(p, False).wait()
-        gath_i[z, p] = nt(halo0[patches + p], blocks[p, 0])
-    for p in range(patches):
-        gath_r[z, p] = rhs[p]
-
-    for copy in map_copies[3:]:
+    for p in range(patches):
+        img[p] = nt(halo0[patches + p], blocks[p, 0])
+
+    for copy in map_copies[3:5]:
         copy.wait()
     for p in range(patches):
         high, low = split(product(nn, sd[p].T, dn[p]))
         gcat[p, 0:terms, :] = high
         gcat[p, terms : 2 * terms, :] = low
-    tall = jnp.concatenate([tr[0, j] for j in range(lists)], axis=1)
-
-    def spot_of(p, j):
-        spot = wrap(neigh[j, p] - (c * patches - patches) + total, total)
-        return jnp.minimum(wrap(spot, total), 3 * patches - 1)
-
-    halo0_copy(0).wait_recv()
-    halo0_copy(1).wait_recv()
-    for p in range(patches):
-        near_copy(p, True).wait()
-        acc = gath_i[z, p]
-        for j in range(1, near_count):
-            acc = acc + nt(halo0[spot_of(p, j)], blocks[p, j])
-        gath_i[z, p] = acc
-        line(lambda t, p=p: image_copy(p, t, z).start())
-
-    def local_of(moments):
-        wide = jnp.concatenate([moments[far[0, j]][:, 0:terms] for j in range(lists)], axis=1)
-        return product(nt, wide, tall)
-
-    plane(lambda s: moment0_copy(s, s).wait_recv())
-    loc_out[...] = jnp.zeros(loc_out.shape, F32)
-    loc_out[:, 0:terms] = local_of(mom0)
-    loc[z] = loc_out[...]
-    line(lambda t: local_copy(t, z).start())
 
     def far_of(local, p):
         high, low = split(local)
@@ -310,28 +324,41 @@
         both = nn(both, gcat[p])
         return both[0:k] + both[k:]
 
+    def spot_of(p, j):
+        spot = wrap(neigh[j, p] - (c * patches - patches) + total, total)
+        return jnp.minimum(wrap(spot, total), 3 * patches - 1)
+
+    for p in range(patches):
+        near_copy(p, True).wait()
+    for side in range(2):
+        for s in range(zs):
+            relay_copy(side, s).wait_recv()
+        join(2 * side)
+    for p in range(patches):
+        acc = img[p]
+        for j in range(1, near_count):
+            acc = acc + nt(halo0[spot_of(p, j)], blocks[p, j])
+        img[p] = acc
+
     line(lambda s: rhs_copy(s, s).wait_recv())
     for p in range(patches):
-        for s in range(zs):
-            img[p, s * cols : (s + 1) * cols, :] = gath_r[s, p]
-        for i, x in enumerate(split3(img[p])):
+        for i, x in enumerate(split3(jnp.concatenate([gath_r[s, p] for s in range(zs)], axis=0))):
             first[p, 2 * i * k : (2 * i + 1) * k, :] = x
 
     line(lambda s: local_copy(s, s).wait_recv())
-    for s in range(zs):
-        base[s * cols : (s + 1) * cols, :] = loc[s]
-    local0 = base[:, 0:terms]
+    local0 = jnp.concatenate([loc[s] for s in range(zs)], axis=0)[:, 0:terms]
     acc1 = jnp.zeros((4 * k, 2 * k), F32)
     acc2 = jnp.zeros((4 * k, 2 * k), F32)
     for p in range(patches):
-        whole = far_of(local0, p)
-        line(lambda s, p=p: image_copy(p, s, s).wait_recv())
-        for s in range(zs):
-            img[p, s * cols : (s + 1) * cols, :] = gath_i[s, p]
-        for i, x in enumerate(split3(img[p] + whole)):
-            first[p, (2 * i + 1) * k : (2 * i + 2) * k, :] = x
-        acc1 = acc1 + nt(first[p, 0 : 4 * k], first[p, 0 : 2 * k])
-        acc2 = acc2 + nt(first[p, 0 : 4 * k], first[p, 2 * k : 4 * k])
+        high, middle, low = split3(img[p] + far_of(local0, p))
+        first[p, k : 2 * k, :] = high
+        first[p, 3 * k : 4 * k, :] = middle
+        first[p, 5 * k : 6 * k, :] = low
+        one = jnp.concatenate([first[p, 0:k], high], axis=0)
+        two = jnp.concatenate([first[p, 2 * k : 3 * k], middle], axis=0)
+        both = jnp.concatenate([one, two], axis=0)
+        acc1 = acc1 + nt(both, one)
+        acc2 = acc2 + nt(both, two)
     gram = acc1[0 : 2 * k] + (acc1[2 * k :] + acc2[0 : 2 * k] + acc2[2 * k :])
     top, low = gram[0:k], gram[k:]
     gram_out[0] = jnp.concatenate(
@@ -353,7 +380,8 @@
             jnp.concatenate([first[p, k : 2 * k], first[p, 3 * k : 4 * k]], axis=0), ucat[p]
         )
     acc = acc[0:k] + acc[k:]
-    momi_out[...] = jnp.concatenate([acc[:, 0:terms] + acc[:, terms:], jnp.zeros_like(acc[:, terms:])], axis=1)
+    acc = acc[:, 0:terms] + acc[:, terms:]
+    momi_out[...] = jnp.concatenate([acc, jnp.zeros((k, 128 - terms), F32)], axis=1)
     momi[c] = momi_out[...]
     plane(lambda t: momenti_copy(t, c).start())
 
@@ -466,13 +494,13 @@
         out[p, cols : 2 * cols, :] = part_r[p] - (both[0:cols] + both[cols:])
 
     for side in range(2):
-        halo0_copy(side).wait_send()
+        for s in range(zs):
+            relay_copy(side, s).wait_send()
         for i in range(chunks):
             halo1_copy(side, i).wait_send()
+    line(lambda t: piece_copy(t, z).wait_send())
     line(lambda t: rhs_copy(t, z).wait_send())
     line(lambda t: local_copy(t, z).wait_send())
-    for p in range(patches):
-        line(lambda t, p=p: image_copy(p, t, z).wait_send())
     plane(lambda t: moment0_copy(t, c).wait_send())
     plane(lambda t: momenti_copy(t, c).wait_send())
     for it in range(2):
@@ -493,7 +521,7 @@
     dma = pltpu.SemaphoreType.DMA
     out = pl.pallas_call(
         functools.partial(kernel, cells, zs, chunks),
-        out_shape=jax.ShapeDtypeStruct((patches, 2 * cols, width), F32),
+        out_shape=pltpu.VMEM((patches, 2 * cols, width), F32),
         in_specs=[hbm, hbm, smem, hbm, hbm, smem, hbm, hbm, hbm],
         out_specs=vmem,
         scratch_shapes=[
@@ -506,7 +534,8 @@
             pltpu.VMEM(dn.shape, F32),
             pltpu.VMEM((patches, 2 * terms, width), BF16),
             pltpu.VMEM((patches, 2 * terms, width), BF16),
-            pltpu.VMEM((3 * patches, cols, width), BF16),
+            pltpu.VMEM((3, zs) + rhs.shape, BF16),
+            pltpu.VMEM((3 * patches, k, width), BF16),
             pltpu.VMEM((3 * patches, k, width), BF16),
             pltpu.VMEM((cols, 128), F32),
             pltpu.VMEM((cells, cols, 128), F32),
@@ -514,7 +543,6 @@
             pltpu.VMEM((cells, k, 128), F32),
             pltpu.VMEM((cols, 128), F32),
             pltpu.VMEM((zs, cols, 128), F32),
-            pltpu.VMEM((zs,) + rhs.shape, F32),
             pltpu.VMEM((zs,) + rhs.shape, F32),
             pltpu.VMEM((k, 128), F32),
             pltpu.VMEM((patches, k, width), F32),
@@ -527,14 +555,14 @@
             pltpu.VMEM((128, k), F32),
             dma((patches, 2)),
             dma((6,)),
-            dma((2,)),
-            dma((2,)),
+            dma((2, zs)),
+            dma((2, zs)),
             dma((cells,)),
             dma((cells,)),
             dma((zs,)),
             dma((zs,)),
-            dma((zs, patches)),
-            dma((zs, patches)),
+            dma((zs,)),
+            dma((zs,)),
             dma((zs,)),
             dma((zs,)),
             dma((2, cells)),

time: 38.3 us -> 35.1 us (0.916)
  Pallas kernels: 35.9 us -> 33.6 us
  local copies, waits for them, and re-layouts: 1.62 us -> 0.65 us
    pallas_call x1, Pallas kernels: 35.9 us -> 33.6 us  [on_device(): pl.pallas_call(functools.partial(kernel, cells, zs, chunks), out_shape=pl...]
    slice x1, local copies, waits for them, and re-layouts: 1.62 us -> 0.65 us  [on_device(): return (out[:, 0:cols], out[:, cols:])]
where the time goes in v3:
time: 35.1 us; the launch traced here: 34.9 us
  Pallas kernels  33.6 us (96%)
  local copies, waits for them, and re-layouts  0.65 us (2%)
  between operations  0.64 us (2%)
    pallas_call x1, Pallas kernels, on_device(): pl.pallas_call(functools.partial(kernel, cells, zs, chunks), out_shape=pl...  33.6 us

profile of v3, /device:TPU:0, one launch (start us, length us, event | category | flops | bytes accessed | tf_op | source)
XLA Modules:
  0.0 34.9 jit_solution(17529118022879209424)
XLA Ops:
  0.6 33.6 %block_cg.1 = f32[8,8,384]{2,1,0:T(8,128)S(1)} custom-call(f32[8,4,384]{2,1,0:T(4,128)} %rhs_hbm.1, bf16[8,4,384,384]{3,2,1,0:T(8,128)(2,1)} %near_hbm.1, s32[4,8]{1,0:T(4,128)} %bitcast.3, f32[8,64,384]{2,1,0:T(8,128)} %up_hbm.1, f32[8,64,64]{2,1,0:T(8,128)} %su_hbm.1, s32[1,4]{1,0:T(1,128)} %far.1, f32[1,4,64,64]{3,2,1,0:T(8,128)} %tr_hbm.1, ...), custom_call_target="tpu_custom_call" | custom-call | tf_op jit(solution)/shard_map/block_cg/pallas_call | solution.py:522
  34.3 0.7 %fusion = (f32[8,4,384]{2,1,0:T(4,128)}, f32[8,4,384]{2,1,0:T(4,128)}) fusion(f32[8,8,384]{2,1,0:T(8,128)S(1)} %block_cg.1), kind=kLoop, calls=%fused_computation | loop fusion | bytes 196608 | tf_op jit(solution)/shard_map/slice | solution.py:580

commit v4 on v3

--- a/solution.py
+++ b/solution.py
@@ -269,6 +269,7 @@
         high, low = split(product(nn, su[p], up[p]))
         ucat[p, 0:terms, :] = high
         ucat[p, terms : 2 * terms, :] = low
+    for p in range(patches):
         acc = acc + nt(rows_of(split(rhs[p])), ucat[p])
     acc = acc[0:cols] + acc[cols:]
     acc = acc[:, 0:terms] + acc[:, terms:]
@@ -347,18 +348,17 @@
 
     line(lambda s: local_copy(s, s).wait_recv())
     local0 = jnp.concatenate([loc[s] for s in range(zs)], axis=0)[:, 0:terms]
+    for p in range(patches):
+        img[p] += far_of(local0, p)
     acc1 = jnp.zeros((4 * k, 2 * k), F32)
     acc2 = jnp.zeros((4 * k, 2 * k), F32)
     for p in range(patches):
-        high, middle, low = split3(img[p] + far_of(local0, p))
-        first[p, k : 2 * k, :] = high
-        first[p, 3 * k : 4 * k, :] = middle
-        first[p, 5 * k : 6 * k, :] = low
-        one = jnp.concatenate([first[p, 0:k], high], axis=0)
-        two = jnp.concatenate([first[p, 2 * k : 3 * k], middle], axis=0)
-        both = jnp.concatenate([one, two], axis=0)
-        acc1 = acc1 + nt(both, one)
-        acc2 = acc2 + nt(both, two)
+        for i, x in enumerate(split3(img[p])):
+            first[p, (2 * i + 1) * k : (2 * i + 2) * k, :] = x
+    for p in range(patches):
+        acc1 = acc1 + nt(first[p, 0 : 4 * k], first[p, 0 : 2 * k])
+    for p in range(patches):
+        acc2 = acc2 + nt(first[p, 0 : 4 * k], first[p, 2 * k : 4 * k])
     gram = acc1[0 : 2 * k] + (acc1[2 * k :] + acc2[0 : 2 * k] + acc2[2 * k :])
     top, low = gram[0:k], gram[k:]
     gram_out[0] = jnp.concatenate(
@@ -435,7 +435,31 @@
     plane(lambda s: momenti_copy(s, s).wait_recv())
     local1 = product(nn, beta1_t, local0) - product(nn, alpha_t, local_of(momi))
     for p in range(patches):
-        img[p] = nt(halo1[patches + p], blocks[p, 0]) + far_of(local1, p)
+        img[p] = nt(halo1[patches + p], blocks[p, 0])
+    for p in range(patches):
+        img[p] += far_of(local1, p)
+    for i in range(chunks):
+        halo1_copy(0, i).wait_recv()
+        halo1_copy(1, i).wait_recv()
+    for p in range(patches):
+        acc = img[p]
+        for j in range(1, near_count):
+            acc = acc + nt(halo1[spot_of(p, j)], blocks[p, j])
+        img[p] = acc
+    acc1 = jnp.zeros((2 * k, k), F32)
+    acc2 = jnp.zeros((k, k), F32)
+    for p in range(patches):
+        high, low = split(img[p])
+        second[p, 2 * k : 3 * k, :] = high
+        second[p, 3 * k : 4 * k, :] = low
+        acc1 = acc1 + nt(second[p, 0 : 2 * k], high)
+        acc2 = acc2 + nt(second[p, 0:k], low)
+    curve = acc1[0:k] + acc1[k:] + acc2
+    gram_out[1] = jnp.concatenate(
+        [0.5 * (curve + curve.T), jnp.zeros((k, 128 - k), F32)], axis=1
+    )
+    grams[1, c] = gram_out[1]
+    plane(lambda t: gram_copy(1, t, c).start())
     mixed = exact(nt, got[:, 5 * k : 6 * k], alpha_t)
     new = (
         got[:, k : 2 * k]
@@ -464,26 +488,6 @@
         part_s[p] = both[0:cols] + both[cols : 2 * cols]
         part_r[p] = rhs[p] - (both[2 * cols : 3 * cols] + both[3 * cols :])
 
-    for i in range(chunks):
-        halo1_copy(0, i).wait_recv()
-        halo1_copy(1, i).wait_recv()
-    acc1 = jnp.zeros((2 * k, k), F32)
-    acc2 = jnp.zeros((k, k), F32)
-    for p in range(patches):
-        acc = img[p]
-        for j in range(1, near_count):
-            acc = acc + nt(halo1[spot_of(p, j)], blocks[p, j])
-        high, low = split(acc)
-        second[p, 2 * k : 3 * k, :] = high
-        second[p, 3 * k : 4 * k, :] = low
-        acc1 = acc1 + nt(second[p, 0 : 2 * k], high)
-        acc2 = acc2 + nt(second[p, 0:k], low)
-    curve = acc1[0:k] + acc1[k:] + acc2
-    gram_out[1] = jnp.concatenate(
-        [0.5 * (curve + curve.T), jnp.zeros((k, 128 - k), F32)], axis=1
-    )
-    grams[1, c] = gram_out[1]
-    plane(lambda t: gram_copy(1, t, c).start())
     (last,) = eliminate([(collect(1) + right, 0)], k)
     turned[...] = last.T
     out_mix = doubled(turned[pl.ds(k + z * cols, cols), :])

time: 35.1 us -> 33.1 us (0.943)
  Pallas kernels: 33.6 us -> 31.6 us
    pallas_call x1, Pallas kernels: 33.6 us -> 31.6 us  [on_device(): pl.pallas_call(functools.partial(kernel, cells, zs, chunks), out_shape=pl...]
where the time goes in v4:
time: 33.1 us; the launch traced here: 32.9 us
  Pallas kernels  31.6 us (95%)
  local copies, waits for them, and re-layouts  0.65 us (2%)
  between operations  0.64 us (2%)
    pallas_call x1, Pallas kernels, on_device(): pl.pallas_call(functools.partial(kernel, cells, zs, chunks), out_shape=pl...  31.6 us

profile of v4, /device:TPU:0, one launch (start us, length us, event | category | flops | bytes accessed | tf_op | source)
XLA Modules:
  0.0 32.9 jit_solution(16918394660744043512)
XLA Ops:
  0.6 31.6 %block_cg.1 = f32[8,8,384]{2,1,0:T(8,128)S(1)} custom-call(f32[8,4,384]{2,1,0:T(4,128)} %rhs_hbm.1, bf16[8,4,384,384]{3,2,1,0:T(8,128)(2,1)} %near_hbm.1, s32[4,8]{1,0:T(4,128)} %bitcast.3, f32[8,64,384]{2,1,0:T(8,128)} %up_hbm.1, f32[8,64,64]{2,1,0:T(8,128)} %su_hbm.1, s32[1,4]{1,0:T(1,128)} %far.1, f32[1,4,64,64]{3,2,1,0:T(8,128)} %tr_hbm.1, ...), custom_call_target="tpu_custom_call" | custom-call | tf_op jit(solution)/shard_map/block_cg/pallas_call | solution.py:526
  32.3 0.7 %fusion = (f32[8,4,384]{2,1,0:T(4,128)}, f32[8,4,384]{2,1,0:T(4,128)}) fusion(f32[8,8,384]{2,1,0:T(8,128)S(1)} %block_cg.1), kind=kLoop, calls=%fused_computation | loop fusion | bytes 196608 | tf_op jit(solution)/shard_map/slice | solution.py:584
